TPU v7x, 32 devices: a whole 2x2x4 slice. The times are simulated.
32 devices in a mesh: prow: 4 (over y, core), pcol: 8 (over z, x).
Axes of the slice: x: 2, y: 2, z: 4, core: 2. Of those that a mesh axis runs over, the one named last changes fastest.
Arguments:
- matrix_slab: float32 [2048, 2048], P('pcol', 'prow'), may hold values from -1024 to 1024
- contributions: float32 [4, 256, 64, 256], P('prow', 'pcol'), may hold values from -3 to 3
- target_column: int32 [4, 256], P('prow', 'pcol'), may hold values from 0 to 31, as said below
- target_rows: int32 [4, 256], P('prow', 'pcol'), may hold values from 0 to 1
- live_rows: int32 [4, 256], P('prow', 'pcol'), may hold values from 1 to 256
- pivot_index: int32 [1, 256], replicated, may hold values from 256 to 2047, as said below
Outputs:
- factored: float32 [2048, 2048], P('pcol', 'prow')
Inputs may be any that keep to these rules, and one draw needn't show every extreme that they name: `pivot_index`: row k lists 256 distinct rows, each (k + 1) * 256 or more. `target_column`: of the 32 blocks held by one device, at most 8 have target column blocks within the columns of one index of pcol, and exactly 8 for some index.
All inputs are finite; a program needn't handle non-finite values.
Results may differ from a plain program's by a relative error of at most 0.0001.
Values sent between devices are 32-bit elements; how exact they have to be, the bound alone decides.
A program may use at most 128 MiB of HBM per device.

v0:
```python
import functools

import jax
import jax.numpy as jnp
from jax import lax
from jax.experimental import pallas as pl
from jax.experimental.pallas import tpu as pltpu
from jax.sharding import PartitionSpec as P

PW = 256
NB = 64
TR = 256
B = 64

HIGHEST = lax.Precision.HIGHEST
VMEM = pltpu.VMEM
F32 = jnp.float32


def hdot(a, b):
    return jnp.dot(a, b, precision=HIGHEST, preferred_element_type=F32)


def spread_kernel(tc, tr, lr, place, blocks, slab, dense):
    cols = slab.shape[0]
    dense[...] = jnp.zeros_like(dense)
    own = pl.multiple_of(place[1] * cols, cols)
    dense[pl.ds(own, cols), :] = slab[...]
    lane = lax.broadcasted_iota(jnp.int32, (NB, TR), 1)

    def add(index, carry):
        c = pl.multiple_of(tc[index] * NB, NB)
        r = pl.multiple_of(tr[index] * TR, TR)
        block = jnp.where(lane < lr[index], blocks[index], 0.0)
        dense[pl.ds(c, NB), pl.ds(r, TR)] += block
        return carry

    lax.fori_loop(0, blocks.shape[0], add, 0)


def eliminate(a):
    groups = B // 8
    eye = (
        lax.broadcasted_iota(jnp.int32, (B, B), 0) == lax.broadcasted_iota(jnp.int32, (B, B), 1)
    ).astype(F32)
    first = jnp.concatenate([a, eye], axis=1)
    second = jnp.concatenate([a.T, eye], axis=1)
    one = [first[8 * g : 8 * g + 8] for g in range(groups)]
    two = [second[8 * g : 8 * g + 8] for g in range(groups)]
    sub = lax.broadcasted_iota(jnp.int32, (8, 2 * B), 0)
    for k in range(B):
        g0, s0 = divmod(k, 8)
        below = sub > s0
        for which, held in enumerate((one, two)):
            col = jnp.broadcast_to(held[g0][:, k : k + 1], (8, 2 * B))
            scaled = jnp.broadcast_to((held[g0] / col)[s0 : s0 + 1, :], (8, 2 * B))
            for g in range(g0 + 1, groups):
                held[g] = held[g] - held[g][:, k : k + 1] * scaled
            fresh = held[g0] - jnp.where(below, col, 0.0) * scaled
            held[g0] = jnp.where(sub == s0, scaled, fresh) if which == 0 else fresh
    first = jnp.concatenate(one, axis=0)
    second = jnp.concatenate(two, axis=0)
    return second[:, :B].T, first[:, :B], first[:, B:], second[:, B:].T


def factor_kernel(source, packed, low_inv, up_inv):
    packed[...] = source[...]
    i = lax.broadcasted_iota(jnp.int32, (B, B), 0)
    j = lax.broadcasted_iota(jnp.int32, (B, B), 1)
    for s in range(0, PW, B):
        e = s + B
        low, up, li, ui = eliminate(packed[s:e, s:e])
        li = jnp.where(i >= j, li, 0.0)
        ui = jnp.where(i <= j, ui, 0.0)
        packed[s:e, s:e] = jnp.where(i >= j, low, up)
        low_inv[s:e, :] = li
        up_inv[s:e, :] = ui
        if e < PW:
            right = hdot(li, packed[s:e, e:])
            left = hdot(packed[e:, s:e], ui)
            packed[s:e, e:] = right
            packed[e:, s:e] = left
            packed[e:, e:] = packed[e:, e:] - hdot(left, right)


def finish_kernel(
    place, pivots, packed, low_inv, up_inv, panel, lead, diag, matrix, incoming, moved, out, x, y
):
    cols, rows = matrix.shape
    row = place[0] * rows + lax.broadcasted_iota(jnp.int32, (PW, rows), 1)
    pick = (pivots[...] == row).astype(F32)
    hit = jnp.sum(pick, axis=0, keepdims=True) > 0.0
    head = place[0] == 0
    x[...] = jnp.where(hit, hdot(lead[...], pick), panel[...])
    x[:, 0:PW] = jnp.where(head, diag[...], x[:, 0:PW])
    for s in range(0, PW, B):
        e = s + B
        part = x[s:e, :]
        if s:
            part = part - hdot(packed[s:e, 0:s], x[0:s, :])
        x[s:e, :] = hdot(low_inv[s:e, :], part)
        part = incoming[:, s:e]
        if s:
            part = part - hdot(y[:, 0:s], packed[0:s, s:e])
        y[:, s:e] = hdot(part, up_inv[s:e, :])
    owners = PW // cols

    @pl.when(place[1] >= owners)
    def _():
        swapped = jnp.where(hit, hdot(moved[...], pick), matrix[...])
        out[...] = swapped - hdot(y[...], x[...])
        out[:, 0:PW] = jnp.where(head, y[...], out[:, 0:PW])

    @pl.when(place[1] < owners)
    def _():
        x[:, 0:PW] = jnp.where(head, packed[...], x[:, 0:PW])
        off = pl.multiple_of(lax.rem(place[1], owners) * cols, cols)
        out[...] = x[pl.ds(off, cols), :]


def shape(*dims):
    return jax.ShapeDtypeStruct(dims, F32)


SMEM_SPEC = pl.BlockSpec(memory_space=pltpu.SMEM)
VMEM_SPEC = pl.BlockSpec(memory_space=pltpu.VMEM)
PARAMS = pltpu.CompilerParams(vmem_limit_bytes=48 * 1024 * 1024)


def per_device(slab_cols, matrix_slab, contributions, target_column, target_rows, live_rows, pivot_index):
    cols, rows = matrix_slab.shape
    row_group = lax.axis_index("prow")
    col_group = lax.axis_index("pcol")
    place = jnp.stack([row_group, col_group]).astype(jnp.int32)
    pivots = pivot_index[0][:, None]
    dense = pl.pallas_call(
        spread_kernel,
        out_shape=shape(slab_cols, rows),
        in_specs=[SMEM_SPEC] * 4 + [VMEM_SPEC] * 2,
        out_specs=VMEM_SPEC,
        compiler_params=PARAMS,
    )(target_column[0], target_rows[0], live_rows[0], place, contributions[0], matrix_slab)
    piece = lax.psum_scatter(dense[0:PW], "pcol", scatter_dimension=0, tiled=True)
    panel = lax.all_gather(piece, "pcol", axis=0, tiled=True)
    global_rows = row_group * rows + jnp.arange(rows)
    pick = (pivots == global_rows[None, :]).astype(F32)
    leading = jnp.concatenate(
        [
            jnp.dot(panel, pick.T, precision=HIGHEST),
            jnp.where(row_group == 0, panel[:, 0:PW], 0.0),
        ],
        axis=0,
    )
    leading = lax.psum(leading, "prow")
    diag, lead = leading[:PW], leading[PW:]
    packed, low_inv, up_inv = pl.pallas_call(
        factor_kernel,
        out_shape=(shape(PW, PW), shape(PW, B), shape(PW, B)),
        in_specs=[VMEM_SPEC],
        out_specs=(VMEM_SPEC,) * 3,
        compiler_params=PARAMS,
        cost_estimate=pl.CostEstimate(flops=10**10, bytes_accessed=10**7, transcendentals=0),
    )(diag)
    matrix = lax.psum_scatter(dense, "pcol", scatter_dimension=0, tiled=True)
    mine = jnp.concatenate(
        [
            jnp.dot(matrix, pick.T, precision=HIGHEST),
            jnp.where(row_group == 0, matrix[:, 0:PW], 0.0),
        ],
        axis=0,
    )
    both = lax.psum(mine, "prow")
    return pl.pallas_call(
        finish_kernel,
        out_shape=shape(cols, rows),
        in_specs=[SMEM_SPEC] + [VMEM_SPEC] * 10,
        out_specs=VMEM_SPEC,
        scratch_shapes=[VMEM((PW, rows), F32), VMEM((cols, PW), F32)],
        compiler_params=PARAMS,
    )(place, pivots, packed, low_inv, up_inv, panel, lead, diag, matrix, both[:cols], both[cols:])


def solution(mesh):
    placed = (
        P("pcol", "prow"),
        P("prow", "pcol", None, None),
        P("prow", "pcol"),
        P("prow", "pcol"),
        P("prow", "pcol"),
        P(),
    )

    def whole(matrix_slab, *rest):
        return jax.shard_map(
            functools.partial(per_device, matrix_slab.shape[0]),
            mesh=mesh,
            in_specs=placed,
            out_specs=P("pcol", "prow"),
            check_vma=False,
        )(matrix_slab, *rest)

    return whole
```

profile of v0, /device:TPU:23, one launch (start us, length us, event | category | flops | bytes accessed | tf_op | source)
XLA Modules:
  0.0 250.8 jit_solution(15273876987975896492)
XLA Ops:
  6.5 0.0 reduce-scatter.3.cloned.1.call-start
  6.5 0.1 pad_add_fusion.place
  6.6 0.0 copy-start.1
  6.6 1.6 copy-done.1
  8.2 0.0 copy-start.2
  8.2 1.0 copy-done.2
  9.2 0.0 copy-start.3
  9.2 0.7 copy-done.3
  9.9 0.0 copy-start.4
  9.9 0.7 copy-done.4
  10.6 0.0 copy-start.5
  10.6 0.7 copy-done.5
  11.2 3.2 %shard_map.64 = f32[2048,512]{1,0:T(8,128)} custom-call(s32[32]{0:T(128)S(1)} %bitcast.11, s32[32]{0:T(128)S(1)} %bitcast.12, s32[32]{0:T(128)S(1)} %bitcast.13, s32[2]{0:T(128)S(1)} %pad_add_fusion.place, f32[32,64,256]{2,1,0:T(8,128)S(1)} %bitcast.10, f32[256,512]{1,0:T(8,128)S(1)} %copy-done.2), custom_call_target="tpu_custom_call" | custom-call | tf_op jit(solution)/shard_map/pallas_call | solution.py:136
  14.4 0.0 copy-start.6
  14.4 1.9 slice.28
  16.3 0.0 reduce-scatter.3.cloned.1.call-update
  16.3 0.0 reduce-scatter.5.cloned.1.call-start
  16.4 0.7 reduce-scatter.5.cloned.1.call-update
  17.1 0.0 all-reduce.3.cloned.1.call-start
  17.2 60.5 %reduce-scatter.3.cloned.1.call-done = f32[32,512]{1,0:T(8,128)} async-done(((f32[256,512]{1,0:T(8,128)}), f32[32,512]{1,0:T(8,128)}) %reduce-scatter.3.cloned.1.call-update) | async-done | bytes 65552 | tf_op jit(solution)/shard_map/reduce_scatter | solution.py:143
  77.7 25.4 %all_gather.3.panel = f32[256,512]{1,0:T(8,128)S(1)} all-gather(f32[32,512]{1,0:T(8,128)} %reduce-scatter.3.cloned.1.call-done), channel_id=1, replica_groups=mesh['prow'=4,'pcol'=8] {'pcol'}, dimensions={0}, use_global_device_ids=true | all-gather | bytes 589824 | tf_op jit(solution)/shard_map/all_gather | solution.py:144
  103.1 0.0 copy-done.6
  103.1 0.5 fusion.2
  103.6 0.8 pad_maximum_fusion
  104.5 69.3 %reduce-scatter.5.cloned.1.call-done.matrix = f32[256,512]{1,0:T(8,128)} async-done(((f32[2048,512]{1,0:T(8,128)}), f32[256,512]{1,0:T(8,128)}) %reduce-scatter.5.cloned.1.call-update) | async-done | bytes 524304 | tf_op jit(solution)/shard_map/reduce_scatter | solution.py:164
  173.7 1.5 fusion
  175.3 1.0 slice_select_fusion
  176.3 0.9 pad_maximum_fusion.1
  177.1 0.0 all-reduce.3.cloned.1.call-update
  177.1 0.1 copy.7.pivots
  177.3 35.8 %all-reduce.3.cloned.1.call-done = (f32[512,256]{1,0:T(8,128)}, f32[512,256]{1,0:T(8,128)}) async-done(((f32[512,256]{1,0:T(8,128)}, f32[512,256]{1,0:T(8,128)}), (f32[512,256]{1,0:T(8,128)}, f32[512,256]{1,0:T(8,128)})) %all-reduce.3.cloned.1.call-update) | async-done | bytes 1048592 | tf_op jit(solution)/shard_map/psum | solution.py:154
  213.0 1.3 fusion.8
  214.3 0.0 copy-start
  214.3 24.0 %shard_map.65 = (f32[256,256]{1,0:T(8,128)S(1)}, f32[256,64]{1,0:T(8,128)S(1)}, f32[256,64]{1,0:T(8,128)S(1)}) custom-call(f32[256,256]{1,0:T(8,128)S(1)} %get-tuple-element.17.source.diag), custom_call_target="tpu_custom_call" | custom-call | flops 10000000000 | bytes 10000000 | tf_op jit(solution)/shard_map/pallas_call | solution.py:156
  238.3 0.0 copy-done
  238.3 6.0 %shard_map.66 = f32[256,512]{1,0:T(8,128)} custom-call(s32[2]{0:T(128)S(1)} %pad_add_fusion.place, s32[256,1]{1,0:T(8,128)S(1)} %copy.7.pivots, f32[256,256]{1,0:T(8,128)S(1)} %get-tuple-element.8.packed, f32[256,64]{1,0:T(8,128)S(1)} %get-tuple-element.9.low_inv, f32[256,64]{1,0:T(8,128)S(1)} %get-tuple-element.10.up_inv, f32[256,512]{1,0:T(8,128)S(1)} %all_gather.3.panel, ...), custom_call_target="tpu_custom_call" | custom-call | tf_op jit(solution)/shard_map/pallas_call | solution.py:173
  (2 shorter events, 0.0 us)
Async XLA Ops:
  6.5 71.1 %reduce-scatter.3.cloned.1.call-start = ((), (), s32[]{:S(2)}) async-start(), calls=%async_computation.2 | async-start | bytes 589824 | tf_op jit(solution)/shard_map/reduce_scatter | solution.py:143
  6.6 1.6 copy-start.1
  8.2 1.0 copy-start.2
  9.2 0.7 copy-start.3
  9.9 0.7 copy-start.4
  10.6 0.7 copy-start.5
  14.4 88.7 %copy-start.6 = (s32[1,256]{1,0:T(1,128)S(1)}, s32[1,256]{1,0:T(1,128)}, u32[]{:S(2)}) copy-start(s32[1,256]{1,0:T(1,128)} %param.11) | copy-start | bytes 3076
  16.3 157.4 %reduce-scatter.5.cloned.1.call-start = ((), (), s32[]{:S(2)}) async-start(), calls=%async_computation.3 | async-start | bytes 4718592 | tf_op jit(solution)/shard_map/reduce_scatter | solution.py:164
  17.1 195.9 %all-reduce.3.cloned.1.call-start = ((), (), s32[]{:S(2)}) async-start(), calls=%async_computation.4 | async-start | bytes 2097152 | tf_op jit(solution)/shard_map/psum | solution.py:154
  214.3 24.0 %copy-start = (f32[256,512]{1,0:T(8,128)S(1)}, f32[256,512]{1,0:T(8,128)}, u32[]{:S(2)}) copy-start(f32[256,512]{1,0:T(8,128)} %reduce-scatter.5.cloned.1.call-done.matrix) | copy-start | bytes 1572868
Sparse Core Ops, SparseCore 0:
  16.5 61.1 reduce-scatter.2
  81.3 92.3 reduce-scatter.4
  177.3 35.7 all-reduce.2
where the time goes:
time: 253 us; the launch traced here: 251 us
  waiting for transfers between devices  166 us (66%)
  Pallas kernels  33.2 us (13%)
  blocking collectives  25.4 us (10%)
  between operations  13.2 us (5%)
  local copies, waits for them, and re-layouts  7.89 us (3%)
  other arithmetic  2.75 us (1%)
    reduce_scatter x1, waiting for transfers between devices, per_device(): matrix = lax.psum_scatter(dense, 'pcol', scatter_dimension=0, tiled=True)  69.3 us
    reduce_scatter x1, waiting for transfers between devices, per_device(): lax.psum_scatter(dense[0:PW], 'pcol', scatter_dimension=0, tiled=True)  60.5 us
    psum x1, waiting for transfers between devices, per_device(): leading = lax.psum(leading, 'prow')  35.8 us
    all_gather x1, blocking collectives, per_device(): panel = lax.all_gather(piece, 'pcol', axis=0, tiled=True)  25.4 us
    pallas_call x1, Pallas kernels, per_device(): pl.pallas_call(factor_kernel, out_shape=(shape(PW, PW), shape(PW, B), sha...  24 us
    pallas_call x1, Pallas kernels, per_device(): pl.pallas_call(finish_kernel, out_shape=shape(cols, rows), in_specs=[SMEM...  6.01 us
  transfers between devices with their start and end apart: 3, of which 3 were waited for; matrix products, arithmetic and copies ran while one was open for 1% of the time, Pallas kernels for 0%

commit v1 on v0

v1 whole, which is shorter than its diff:
```python
import functools

import jax
import jax.numpy as jnp
from jax import lax
from jax.experimental import pallas as pl
from jax.experimental.pallas import tpu as pltpu
from jax.sharding import PartitionSpec as P

PW = 256
NB = 64
TR = 256
B = 64
AHEAD = 4

HIGHEST = lax.Precision.HIGHEST
VMEM = pltpu.VMEM
F32 = jnp.float32
MESH = pl.DeviceIdType.MESH


def hdot(a, b):
    return jnp.dot(a, b, precision=HIGHEST, preferred_element_type=F32)


def hdot_t(a, b):
    return lax.dot_general(a, b, (((1,), (1,)), ((), ())), precision=HIGHEST, preferred_element_type=F32)


def pick_matrix(pivots, group, rows):
    row = group * rows + lax.broadcasted_iota(jnp.int32, (rows, PW), 0)
    return (row == pivots[...]).astype(F32)


def spread_kernel(tc, tr, lr, blocks, slab, pivots, dense, sel, tcs, trs, lrs, held, own_slab, sem):
    cols, rows = own_slab.shape
    count = held.shape[0]
    parts = sem.shape[0] - 4
    size = count // parts
    tables = [pltpu.make_async_copy(a, b, sem.at[i]) for i, (a, b) in enumerate(((tc, tcs), (tr, trs), (lr, lrs)))]
    rest = pltpu.make_async_copy(slab, own_slab, sem.at[3])
    pieces = [
        pltpu.make_async_copy(
            blocks.at[0, pl.ds(i * size, size)], held.at[pl.ds(i * size, size)], sem.at[4 + i]
        )
        for i in range(parts)
    ]
    for copy in tables + pieces + [rest]:
        copy.start()
    dense[...] = jnp.zeros_like(dense)
    pick = pick_matrix(pivots, lax.axis_index("prow"), rows)
    lane = lax.broadcasted_iota(jnp.int32, (NB, TR), 1)
    for copy in tables:
        copy.wait()

    def add(index, carry):
        c = pl.multiple_of(tcs[0, index] * NB, NB)
        r = pl.multiple_of(trs[0, index] * TR, TR)
        block = jnp.where(lane < lrs[0, index], held[index], 0.0)
        dense[pl.ds(c, NB), pl.ds(r, TR)] += block
        return carry

    for i in range(parts):
        pieces[i].wait()
        lax.fori_loop(i * size, (i + 1) * size, add, 0)
    rest.wait()
    own = pl.multiple_of(lax.axis_index("pcol") * cols, cols)
    dense[pl.ds(own, cols), :] += own_slab[...]
    sel[...] = hdot(dense[0:PW, :], pick)


def eliminate(a, every=4):
    groups = B // 8
    eye = (
        lax.broadcasted_iota(jnp.int32, (B, B), 0) == lax.broadcasted_iota(jnp.int32, (B, B), 1)
    ).astype(F32)
    first = jnp.concatenate([a, eye], axis=1)
    second = jnp.concatenate([a.T, eye], axis=1)
    one = [first[8 * g : 8 * g + 8] for g in range(groups)]
    two = [second[8 * g : 8 * g + 8] for g in range(groups)]
    sub = lax.broadcasted_iota(jnp.int32, (8, 2 * B), 0)
    for k in range(B):
        g0, s0 = divmod(k, 8)
        below = sub > s0
        for which, held in enumerate((one, two)):
            col = jnp.broadcast_to(held[g0][:, k : k + 1], (8, 2 * B))
            scaled = jnp.broadcast_to((held[g0] / col)[s0 : s0 + 1, :], (8, 2 * B))
            for g in range(g0 + 1, groups):
                held[g] = held[g] - held[g][:, k : k + 1] * scaled
            fresh = held[g0] - jnp.where(below, col, 0.0) * scaled
            held[g0] = jnp.where(sub == s0, scaled, fresh) if which == 0 else fresh
        if k % every == every - 1:
            yield None
    first = jnp.concatenate(one, axis=0)
    second = jnp.concatenate(two, axis=0)
    return second[:, :B].T, first[:, :B], first[:, B:], second[:, B:].T


def factor(packed, low_inv, up_inv):
    i = lax.broadcasted_iota(jnp.int32, (B, B), 0)
    j = lax.broadcasted_iota(jnp.int32, (B, B), 1)
    for s in range(0, PW, B):
        e = s + B
        low, up, li, ui = yield from eliminate(packed[s:e, s:e])
        li = jnp.where(i >= j, li, 0.0)
        ui = jnp.where(i <= j, ui, 0.0)
        packed[s:e, s:e] = jnp.where(i >= j, low, up)
        low_inv[s:e, :] = li
        up_inv[s:e, :] = ui
        if e < PW:
            right = hdot(li, packed[s:e, e:])
            left = hdot(packed[e:, s:e], ui)
            packed[s:e, e:] = right
            packed[e:, s:e] = left
            packed[e:, e:] = packed[e:, e:] - hdot(left, right)
        yield None


def main_kernel(
    n_row, n_col,
    pivots, dense, sel, out,
    diag_in, diag, panel_in, panel, lead, xr, zl, zr, final, mine, others, moved, pick, packed, low_inv, up_inv,
    x, y,
    diag_sem, panel_sem, lead_sem, x_sem, z_sem, row_sem, moved_sem,
):
    n = n_row * n_col
    cols, rows = out.shape
    group, place = lax.axis_index("prow"), lax.axis_index("pcol")
    me = group * n_col + place
    owners = PW // cols
    per = cols // NB
    reducers, piece = diag.shape[0] // diag_in.shape[1], diag_in.shape[1]
    part = panel_in.shape[1]
    depth = n_col // 2
    level, side = lax.div(place, 2), lax.rem(place, 2)
    steps = depth * per
    half = lax.div(level, depth // 2)

    def device(index):
        return (lax.div(index, n_col), lax.rem(index, n_col))

    def local(ref, sem):
        return pltpu.make_async_copy(ref, ref, sem)

    def send(src, dst, ss, rs, where):
        return pltpu.make_async_remote_copy(
            src_ref=src, dst_ref=dst, send_sem=ss, recv_sem=rs, device_id=where, device_id_type=MESH
        )

    barrier = pltpu.get_barrier_semaphore()

    def greet(d, carry):
        pl.semaphore_signal(barrier, inc=1, device_id=device(lax.rem(me + d, n)), device_id_type=MESH)
        return carry

    lax.fori_loop(1, n, greet, 0)
    pick[...] = pick_matrix(pivots, group, rows)
    pl.semaphore_wait(barrier, n - 1)

    def diag_send(d, carry):
        t = lax.rem(me + d, n)

        def go():
            at = pl.multiple_of(t * piece, piece)
            send(sel.at[pl.ds(at, piece)], diag_in.at[d - 1], diag_sem.at[0], diag_sem.at[1], device(t)).start()

        if reducers == n:
            go()
        else:
            pl.when(t < reducers)(go)
        return carry

    def if_reducer(f):
        if reducers == n:
            f()
        else:
            pl.when(me < reducers)(f)

    def if_not_reducer(f):
        if reducers != n:
            pl.when(me >= reducers)(f)

    lax.fori_loop(1, n, diag_send, 0)

    def x_where(k):
        zone, c = divmod(k, per)
        return half * zone + (1 - half) * (depth - 1 - zone), c

    def x_copy(k):
        goal, c = x_where(k)
        owner = goal * 2 + 1 - side
        at = pl.multiple_of(owner * cols + c * NB, NB)
        copy = send(
            dense.at[pl.ds(at, NB)], xr.at[k], x_sem.at[0, k], x_sem.at[1, k], (group, place + 1 - 2 * side)
        )
        return owner >= owners, copy

    def x_send(k):
        if k < steps:
            live, copy = x_copy(k)
            pl.when(live)(copy.start)

    x_send(0)

    @if_reducer
    def _():
        local(diag_in, diag_sem.at[1]).wait()
        at = pl.multiple_of(me * piece, piece)
        diag[pl.ds(at, piece), :] = sel[pl.ds(at, piece), :] + jnp.sum(diag_in[...], axis=0)

        def diag_spread(d, carry):
            own = diag.at[pl.ds(at, piece)]
            send(own, own, diag_sem.at[2], diag_sem.at[3], device(lax.rem(me + d, n))).start()
            return carry

        lax.fori_loop(1, n, diag_spread, 0)

    def panel_send(d, carry):
        t = lax.rem(place + d, n_col)
        at = pl.multiple_of(t * part, part)
        send(dense.at[pl.ds(at, part)], panel_in.at[d - 1], panel_sem.at[0], panel_sem.at[1], (group, t)).start()
        return carry

    lax.fori_loop(1, n_col, panel_send, 0)
    part_at = pl.multiple_of(place * part, part)

    def panel_reduce():
        local(panel_in, panel_sem.at[1]).wait()
        panel[pl.ds(part_at, part), :] = dense[pl.ds(part_at, part), :] + jnp.sum(panel_in[...], axis=0)

        def panel_spread(d, carry):
            own = panel.at[pl.ds(part_at, part)]
            t = lax.rem(place + d, n_col)
            send(own, own, panel_sem.at[2], panel_sem.at[3], (group, t)).start()
            return carry

        lax.fori_loop(1, n_col, panel_spread, 0)

    def lead_copy(d):
        return send(panel.at[:, 0:PW], lead, lead_sem.at[0, d], lead_sem.at[1, 0], (lax.rem(group + d, n_row), place))

    def panel_finish():
        local(panel.at[pl.ds(0, (n_col - 1) * part)], panel_sem.at[3]).wait()

        @pl.when(group == 0)
        def _():
            for d in range(1, n_row):
                lead_copy(d).start()

    def z_copy(k, way):
        goal, c = x_where(k)
        slot = goal * per + c
        into = zl if way > 0 else zr
        return send(
            xr.at[k], into.at[slot], z_sem.at[0, slot], z_sem.at[1 if way > 0 else 2, slot], (group, place + 2 * way)
        )

    def row_copy(c, d):
        return send(
            mine.at[c], others.at[c, d - 1], row_sem.at[0, c], row_sem.at[1, c], (lax.rem(group + d, n_row), place)
        )

    def moved_copy(c, d):
        return send(
            final.at[c, :, 0:PW], moved.at[c], moved_sem.at[0, c], moved_sem.at[1, c],
            (lax.rem(group + d, n_row), place),
        )

    def chunk(k):
        goal, c = x_where(k)
        owner = goal * 2 + side
        slot = goal * per + c

        @pl.when(owner >= owners)
        def _():
            x_copy(k)[1].wait_recv()
            at = pl.multiple_of(owner * cols + c * NB, NB)
            xr[k] = xr[k] + dense[pl.ds(at, NB), :]

            @pl.when((level <= goal) & (level > 0))
            def _():
                pltpu.make_async_copy(zl.at[slot], zl.at[slot], z_sem.at[1, slot]).wait()
                xr[k] = xr[k] + zl[slot]

            @pl.when((level >= goal) & (level < depth - 1))
            def _():
                pltpu.make_async_copy(zr.at[slot], zr.at[slot], z_sem.at[2, slot]).wait()
                xr[k] = xr[k] + zr[slot]

            @pl.when(level < goal)
            def _():
                z_copy(k, 1).start()

            @pl.when(level > goal)
            def _():
                z_copy(k, -1).start()

            @pl.when(level == goal)
            def _():
                final[c] = xr[k]
                mine[c] = hdot(xr[k], pick[...])
                for d in range(1, n_row):
                    row_copy(c, d).start()

                @pl.when(group == 0)
                def _():
                    for d in range(1, n_row):
                        moved_copy(c, d).start()

    for k in range(1, AHEAD):
        x_send(k)
    chunk(0)
    x_send(AHEAD)
    kept = (reducers - 1) * piece
    local(diag.at[pl.ds(0, kept)], diag_sem.at[3]).wait()
    if_not_reducer(lambda: local(diag.at[pl.ds(0, piece)], diag_sem.at[3]).wait())
    packed[...] = diag[...]
    work = factor(packed, low_inv, up_inv)
    total = (B // 4 + 1) * (PW // B)
    pace = -(-total // (steps - 1))
    for k in range(1, steps):
        chunk(k)
        x_send(k + AHEAD)
        if k == 3:
            panel_reduce()
        if k == 8:
            panel_finish()
        for _ in range(pace):
            next(work, None)
    for _ in work:
        pass

    @pl.when(group > 0)
    def _():
        local(lead, lead_sem.at[1, 0]).wait()

    @pl.when(group == 0)
    def _():
        lead[...] = panel[:, 0:PW]

    head = group == 0
    hit = hdot_t(jnp.ones((8, PW), F32), pick[...])[0:1, :] > 0.5
    x[...] = jnp.where(hit, hdot_t(lead[...], pick[...]), panel[...])
    x[:, 0:PW] = jnp.where(head, diag[...], x[:, 0:PW])
    for s in range(0, PW, B):
        e = s + B
        term = x[s:e, :]
        if s:
            term = term - hdot(packed[s:e, 0:s], x[0:s, :])
        x[s:e, :] = hdot(low_inv[s:e, :], term)

    @pl.when(place >= owners)
    def _():
        for c in range(per):
            local(others.at[c], row_sem.at[1, c]).wait()

            @pl.when(group > 0)
            def _():
                local(moved.at[c], moved_sem.at[1, c]).wait()

            @pl.when(group == 0)
            def _():
                moved[c] = final[c, :, 0:PW]

            mine_all = mine[c] + jnp.sum(others[c], axis=0)
            for s in range(0, PW, B):
                e = s + B
                term = mine_all[:, s:e]
                if s:
                    term = term - hdot(y[:, 0:s], packed[0:s, s:e])
                y[:, s:e] = hdot(term, up_inv[s:e, :])
            swapped = jnp.where(hit, hdot_t(moved[c], pick[...]), final[c])
            lo = c * NB
            out[lo : lo + NB, :] = swapped - hdot(y[...], x[...])
            out[lo : lo + NB, 0:PW] = jnp.where(head, y[...], out[lo : lo + NB, 0:PW])

    @pl.when(place < owners)
    def _():
        x[:, 0:PW] = jnp.where(head, packed[...], x[:, 0:PW])
        off = pl.multiple_of(lax.rem(place, owners) * cols, cols)
        out[...] = x[pl.ds(off, cols), :]

    local(diag.at[pl.ds(0, kept)], diag_sem.at[0]).wait()
    if_not_reducer(lambda: local(diag.at[pl.ds(0, piece)], diag_sem.at[0]).wait())
    if_reducer(lambda: local(diag_in, diag_sem.at[2]).wait())
    local(panel_in, panel_sem.at[0]).wait()
    local(panel_in, panel_sem.at[2]).wait()

    @pl.when(group == 0)
    def _():
        for d in range(1, n_row):
            lead_copy(d).wait_send()

    for k in range(steps):
        live, copy = x_copy(k)
        pl.when(live)(copy.wait_send)
        goal, c = x_where(k)

        @pl.when((goal * 2 + side >= owners) & (level != goal))
        def _():
            z_copy(k, 1).wait_send()

    @pl.when(place >= owners)
    def _():
        for c in range(per):
            local(others.at[c], row_sem.at[0, c]).wait()

            @pl.when(group == 0)
            def _():
                local(others.at[c], moved_sem.at[0, c]).wait()


def shape(*dims):
    return jax.ShapeDtypeStruct(dims, F32)


HBM_SPEC = pl.BlockSpec(memory_space=pltpu.MemorySpace.HBM)
VMEM_SPEC = pl.BlockSpec(memory_space=pltpu.VMEM)
DMA = pltpu.SemaphoreType.DMA


def per_device(
    n_row, n_col, matrix_slab, contributions, target_column, target_rows, live_rows, pivot_index
):
    cols, rows = matrix_slab.shape
    slab_cols = cols * n_col
    count = contributions.shape[1]
    n = n_row * n_col
    parts = 4
    table = pltpu.SMEM((1, count), jnp.int32)
    dense, sel = pl.pallas_call(
        spread_kernel,
        out_shape=(shape(slab_cols, rows), shape(PW, PW)),
        in_specs=[HBM_SPEC] * 5 + [VMEM_SPEC],
        out_specs=(VMEM_SPEC,) * 2,
        scratch_shapes=[table] * 3
        + [VMEM((count, NB, TR), F32), VMEM((cols, rows), F32), DMA((4 + parts,))],
        compiler_params=pltpu.CompilerParams(vmem_limit_bytes=32 * 1024 * 1024),
    )(target_column, target_rows, live_rows, contributions, matrix_slab, pivot_index)
    piece = max(8, PW // n)
    per = cols // NB
    depth = n_col // 2
    steps = depth * per
    part = PW // n_col
    scratch = [
        VMEM((n - 1, piece, PW), F32),
        VMEM((PW, PW), F32),
        VMEM((n_col - 1, part, rows), F32),
        VMEM((PW, rows), F32),
        VMEM((PW, PW), F32),
        VMEM((steps, NB, rows), F32),
        VMEM((steps, NB, rows), F32),
        VMEM((steps, NB, rows), F32),
        VMEM((per, NB, rows), F32),
        VMEM((per, NB, PW), F32),
        VMEM((per, n_row - 1, NB, PW), F32),
        VMEM((per, NB, PW), F32),
        VMEM((rows, PW), F32),
        VMEM((PW, PW), F32),
        VMEM((PW, B), F32),
        VMEM((PW, B), F32),
        VMEM((PW, rows), F32),
        VMEM((NB, PW), F32),
        DMA((4,)),
        DMA((4,)),
        DMA((2, n_row)),
        DMA((2, steps)),
        DMA((3, steps)),
        DMA((2, per)),
        DMA((2, per)),
    ]
    return pl.pallas_call(
        functools.partial(main_kernel, n_row, n_col),
        out_shape=shape(cols, rows),
        in_specs=[VMEM_SPEC] * 3,
        out_specs=VMEM_SPEC,
        scratch_shapes=scratch,
        compiler_params=pltpu.CompilerParams(
            collective_id=0, has_side_effects=True, vmem_limit_bytes=32 * 1024 * 1024
        ),
    )(pivot_index, dense, sel)


def solution(mesh):
    placed = (
        P("pcol", "prow"),
        P("prow", "pcol", None, None),
        P("prow", "pcol"),
        P("prow", "pcol"),
        P("prow", "pcol"),
        P(),
    )
    body = functools.partial(per_device, mesh.shape["prow"], mesh.shape["pcol"])

    def whole(*args):
        return jax.shard_map(
            body, mesh=mesh, in_specs=placed, out_specs=P("pcol", "prow"), check_vma=False
        )(*args)

    return whole
```

time: 253 us -> 106 us (0.42)
  the two profiles are of different devices: /device:TPU:23 before, /device:TPU:2 now
where the time goes in v1:
time: 106 us
  Pallas kernels  99.7 us (94%)
  local copies, waits for them, and re-layouts  6.07 us (6%)
    pallas_call x1, Pallas kernels, per_device(): pl.pallas_call(functools.partial(main_kernel, n_row, n_col), out_shape=sh...  98 us
    unnamed x13, local copies, waits for them, and re-layouts  6.07 us

profile of v1, /device:TPU:2, one launch (start us, length us, event | category | flops | bytes accessed | tf_op | source)
XLA Modules:
  0.0 105.8 jit_solution(16177047212259936763)
XLA Ops:
  0.0 0.0 copy-start
  0.0 1.6 %copy-done = f32[1,32,64,256]{3,2,1,0:T(8,128)S(1)} copy-done((f32[1,32,64,256]{3,2,1,0:T(8,128)S(1)}, f32[1,32,64,256]{3,2,1,0:T(8,128)}, u32[]{:S(2)}) %copy-start) | copy-done | bytes 2097176
  1.6 0.0 copy-start.1
  1.6 1.0 copy-done.1
  2.6 0.0 copy-start.2
  2.6 0.7 copy-done.2
  3.3 0.0 copy-start.3
  3.3 0.7 copy-done.3
  4.0 0.0 copy-start.4
  4.0 0.7 copy-done.4
  4.6 0.0 copy-start.5
  4.6 0.7 copy-done.5
  5.3 1.7 %shard_map.64 = (f32[2048,512]{1,0:T(8,128)S(1)}, f32[256,256]{1,0:T(8,128)S(1)}) custom-call(s32[1,32]{1,0:T(1,128)S(1)} %copy-done.3, s32[1,32]{1,0:T(1,128)S(1)} %copy-done.4, s32[1,32]{1,0:T(1,128)S(1)} %copy-done.5, f32[1,32,64,256]{3,2,1,0:T(8,128)S(1)} %copy-done, f32[256,512]{1,0:T(8,128)S(1)} %copy-done.1, s32[1,256]{1,0:T(1,128)S(1)} %copy-done.2), custom_call_target="tpu_custom_call" | custom-call | tf_op jit(solution)/shard_map/pallas_call | solution.py:431
  7.0 98.0 %shard_map.65 = f32[256,512]{1,0:T(8,128)S(1)} custom-call(s32[1,256]{1,0:T(1,128)S(1)} %copy-done.2, f32[2048,512]{1,0:T(8,128)S(1)} %get-tuple-element.7.dense, f32[256,256]{1,0:T(8,128)S(1)} %get-tuple-element.8.sel), custom_call_target="tpu_custom_call" | custom-call | tf_op jit(solution)/shard_map/pallas_call | solution.py:472
  105.0 0.8 copy.8
Async XLA Ops:
  0.0 1.6 %copy-start = (f32[1,32,64,256]{3,2,1,0:T(8,128)S(1)}, f32[1,32,64,256]{3,2,1,0:T(8,128)}, u32[]{:S(2)}) copy-start(f32[1,32,64,256]{3,2,1,0:T(8,128)} %blocks.1) | copy-start | bytes 6291460
  1.6 1.0 copy-start.1
  2.6 0.7 copy-start.2
  3.3 0.7 copy-start.3
  4.0 0.7 copy-start.4
  4.6 0.7 copy-start.5

commit v2 on v1

v2 whole, which is shorter than its diff:
```python
import functools

import jax
import jax.numpy as jnp
from jax import lax
from jax.experimental import pallas as pl
from jax.experimental.pallas import tpu as pltpu
from jax.sharding import PartitionSpec as P

PW = 256
NB = 64
TR = 256
B = 64
LAG = 3

HIGHEST = lax.Precision.HIGHEST
VMEM = pltpu.VMEM
F32 = jnp.float32
MESH = pl.DeviceIdType.MESH


def hdot(a, b):
    return jnp.dot(a, b, precision=HIGHEST, preferred_element_type=F32)


def hdot_t(a, b):
    return lax.dot_general(a, b, (((1,), (1,)), ((), ())), precision=HIGHEST, preferred_element_type=F32)


def pick_matrix(pivots, group, rows):
    row = group * rows + lax.broadcasted_iota(jnp.int32, (rows, PW), 0)
    return (row == pivots[...]).astype(F32)


def spread_kernel(tc, tr, lr, blocks, slab, pivots, dense, sel, tcs, trs, lrs, held, own_slab, pivot_row, sem):
    cols, rows = own_slab.shape
    count = held.shape[0]
    parts = sem.shape[0] - 5
    size = count // parts
    tables = [pltpu.make_async_copy(a, b, sem.at[i]) for i, (a, b) in enumerate(((tc, tcs), (tr, trs), (lr, lrs)))]
    rest = pltpu.make_async_copy(slab, own_slab, sem.at[3])
    order = pltpu.make_async_copy(pivots, pivot_row, sem.at[4])
    pieces = [
        pltpu.make_async_copy(
            blocks.at[0, pl.ds(i * size, size)], held.at[pl.ds(i * size, size)], sem.at[5 + i]
        )
        for i in range(parts)
    ]
    for copy in tables + pieces + [rest, order]:
        copy.start()
    dense[...] = jnp.zeros_like(dense)
    lane = lax.broadcasted_iota(jnp.int32, (NB, TR), 1)
    for copy in tables:
        copy.wait()

    def add(index, carry):
        c = pl.multiple_of(tcs[0, index] * NB, NB)
        r = pl.multiple_of(trs[0, index] * TR, TR)
        block = jnp.where(lane < lrs[0, index], held[index], 0.0)
        dense[pl.ds(c, NB), pl.ds(r, TR)] += block
        return carry

    for i in range(parts):
        pieces[i].wait()
        lax.fori_loop(i * size, (i + 1) * size, add, 0)
    rest.wait()
    own = pl.multiple_of(lax.axis_index("pcol") * cols, cols)
    dense[pl.ds(own, cols), :] += own_slab[...]
    order.wait()
    sel[...] = hdot(dense[0:PW, :], pick_matrix(pivot_row, lax.axis_index("prow"), rows))


def eliminate(a, every=4):
    groups = B // 8
    eye = (
        lax.broadcasted_iota(jnp.int32, (B, B), 0) == lax.broadcasted_iota(jnp.int32, (B, B), 1)
    ).astype(F32)
    first = jnp.concatenate([a, eye], axis=1)
    second = jnp.concatenate([a.T, eye], axis=1)
    one = [first[8 * g : 8 * g + 8] for g in range(groups)]
    two = [second[8 * g : 8 * g + 8] for g in range(groups)]
    sub = lax.broadcasted_iota(jnp.int32, (8, 2 * B), 0)
    for k in range(B):
        g0, s0 = divmod(k, 8)
        below = sub > s0
        for which, held in enumerate((one, two)):
            col = jnp.broadcast_to(held[g0][:, k : k + 1], (8, 2 * B))
            scaled = jnp.broadcast_to((held[g0] / col)[s0 : s0 + 1, :], (8, 2 * B))
            for g in range(g0 + 1, groups):
                held[g] = held[g] - held[g][:, k : k + 1] * scaled
            fresh = held[g0] - jnp.where(below, col, 0.0) * scaled
            held[g0] = jnp.where(sub == s0, scaled, fresh) if which == 0 else fresh
        if k % every == every - 1:
            yield None
    first = jnp.concatenate(one, axis=0)
    second = jnp.concatenate(two, axis=0)
    return second[:, :B].T, first[:, :B], first[:, B:], second[:, B:].T


def factor(packed, low_inv, up_inv):
    i = lax.broadcasted_iota(jnp.int32, (B, B), 0)
    j = lax.broadcasted_iota(jnp.int32, (B, B), 1)
    for s in range(0, PW, B):
        e = s + B
        low, up, li, ui = yield from eliminate(packed[s:e, s:e])
        li = jnp.where(i >= j, li, 0.0)
        ui = jnp.where(i <= j, ui, 0.0)
        packed[s:e, s:e] = jnp.where(i >= j, low, up)
        low_inv[s:e, :] = li
        up_inv[s:e, :] = ui
        if e < PW:
            right = hdot(li, packed[s:e, e:])
            left = hdot(packed[e:, s:e], ui)
            packed[s:e, e:] = right
            packed[e:, s:e] = left
            packed[e:, e:] = packed[e:, e:] - hdot(left, right)
        yield None


def main_kernel(
    n_row, n_col,
    pivots, dense, sel, out,
    block_in, block, piece_in, diag, half_in, part_in, panel, lead, xr, zl, zr,
    final, mine, pair_in, others, moved, pick, packed, low_inv, up_inv, x, y,
    pivot_row, pivot_sem, diag_sem, panel_sem, lead_sem, x_sem, z_sem, pair_sem, row_sem, moved_sem,
):
    cols, rows = out.shape
    group, place = lax.axis_index("prow"), lax.axis_index("pcol")
    me = group * n_col + place
    n = n_row * n_col
    owners = PW // cols
    per = cols // NB
    wide = block.shape[0]
    piece = piece_in.shape[1]
    reducers = wide // piece
    pairs = n_row // 2
    depth = n_col // 2
    part = part_in.shape[1]
    steps = depth * per
    level, side = lax.div(place, 2), lax.rem(place, 2)
    row, core = lax.div(group, 2), lax.rem(group, 2)
    near = depth // 2
    half = lax.div(level, near)
    across = (group, place + 1 - 2 * side)
    partner = (group + 1 - 2 * core, place)

    def local(ref, sem):
        return pltpu.make_async_copy(ref, ref, sem)

    def send(src, dst, ss, rs, where):
        return pltpu.make_async_remote_copy(
            src_ref=src, dst_ref=dst, send_sem=ss, recv_sem=rs, device_id=where, device_id_type=MESH
        )

    def rows_of(ref, start, size):
        return ref.at[pl.ds(pl.multiple_of(start, size), size)]

    pivot_copy = pltpu.make_async_copy(pivots, pivot_row, pivot_sem)
    pivot_copy.start()
    barrier = pltpu.get_barrier_semaphore()

    def greet(d, carry):
        t = lax.rem(me + d, n)
        pl.semaphore_signal(
            barrier, inc=1, device_id=(lax.div(t, n_col), lax.rem(t, n_col)), device_id_type=MESH
        )
        return carry

    lax.fori_loop(1, n, greet, 0)
    pivot_copy.wait()
    pick[...] = pick_matrix(pivot_row, group, rows)
    pl.semaphore_wait(barrier, n - 1)

    for d in range(1, n_row):
        t = lax.rem(group + d, n_row)
        send(rows_of(sel, t * wide, wide), block_in.at[d - 1], diag_sem.at[0], diag_sem.at[1], (t, place)).start()
    keep = PW // 2
    half_copy = send(
        rows_of(dense, (1 - side) * keep, keep), half_in, panel_sem.at[0], panel_sem.at[1], across
    )
    half_copy.start()

    def x_where(k):
        zone, c = divmod(k, per)
        if zone < near:
            return half * zone + (1 - half) * (depth - 1 - zone), c
        return half * near + lax.rem(level - half * near + 1 + zone - near, near), c

    def x_copy(k):
        goal, c = x_where(k)
        owner = goal * 2 + 1 - side
        src = rows_of(dense, owner * cols + c * NB, NB)
        return owner >= owners, send(src, xr.at[k], x_sem.at[0, k], x_sem.at[1, k], across)

    def x_send(k):
        if k < steps:
            live, copy = x_copy(k)
            pl.when(live)(copy.start)

    def if_reducer(f):
        if reducers == n_col:
            f()
        else:
            pl.when(place < reducers)(f)

    def if_not_reducer(f):
        if reducers != n_col:
            pl.when(place >= reducers)(f)

    local(block_in, diag_sem.at[1]).wait()
    at = pl.multiple_of(group * wide, wide)
    block[...] = sel[pl.ds(at, wide), :] + jnp.sum(block_in[...], axis=0)

    def piece_send(d, carry):
        t = lax.rem(place + d, n_col)

        def go():
            send(
                rows_of(block, t * piece, piece), piece_in.at[d - 1], diag_sem.at[2], diag_sem.at[3], (group, t)
            ).start()

        if reducers == n_col:
            go()
        else:
            pl.when(t < reducers)(go)
        return carry

    lax.fori_loop(1, n_col, piece_send, 0)
    x_send(0)

    def panel_middle():
        half_copy.wait_recv()
        at = pl.multiple_of(side * keep, keep)
        half_in[...] = half_in[...] + dense[pl.ds(at, keep), :]
        for d in range(1, depth):
            t = lax.rem(level + d, depth)
            send(
                rows_of(half_in, t * part, part), part_in.at[d - 1], panel_sem.at[2], panel_sem.at[3],
                (group, t * 2 + side),
            ).start()

    part_at = pl.multiple_of(side * keep + level * part, part)
    twin_at = pl.multiple_of((1 - side) * keep + level * part, part)

    def panel_sum():
        local(part_in, panel_sem.at[3]).wait()
        mid = pl.multiple_of(level * part, part)
        panel[pl.ds(part_at, part), :] = half_in[pl.ds(mid, part), :] + jnp.sum(part_in[...], axis=0)
        panel_twin(part_at).start()
        panel_spread(part_at, 4)

    def panel_twin(at):
        own = panel.at[pl.ds(at, part)]
        return send(own, own, panel_sem.at[6], panel_sem.at[7], across)

    def panel_spread(at, sem):
        own = panel.at[pl.ds(at, part)]
        for d in range(1, depth):
            t = lax.rem(level + d, depth)
            send(own, own, panel_sem.at[sem], panel_sem.at[sem + 1], (group, t * 2 + side)).start()

    def panel_gather():
        panel_twin(twin_at).wait_recv()
        panel_spread(twin_at, 8)

    def lead_copy(d):
        return send(
            panel.at[:, 0:PW], lead, lead_sem.at[0, d], lead_sem.at[1, 0], (lax.rem(group + d, n_row), place)
        )

    def panel_finish():
        local(part_in, panel_sem.at[5]).wait()
        local(part_in, panel_sem.at[9]).wait()

        @pl.when(group == 0)
        def _():
            for d in range(1, n_row):
                lead_copy(d).start()

    panel_middle()
    diag_at = pl.multiple_of(group * wide + place * piece, piece)

    @if_reducer
    def _():
        local(piece_in, diag_sem.at[3]).wait()
        mid = pl.multiple_of(place * piece, piece)
        diag[pl.ds(diag_at, piece), :] = block[pl.ds(mid, piece), :] + jnp.sum(piece_in[...], axis=0)

        def piece_spread(d, carry):
            own = diag.at[pl.ds(diag_at, piece)]
            send(own, own, diag_sem.at[4], diag_sem.at[5], (group, lax.rem(place + d, n_col))).start()
            return carry

        lax.fori_loop(1, n_col, piece_spread, 0)

    x_send(1)
    x_send(2)

    def z_copy(k, way):
        goal, c = x_where(k)
        slot = goal * per + c
        into = zl if way > 0 else zr
        return send(
            xr.at[k], into.at[slot], z_sem.at[0, slot], z_sem.at[1 if way > 0 else 2, slot], (group, place + 2 * way)
        )

    def pair_copy(c):
        return send(mine.at[pl.ds(c * NB, NB)], pair_in.at[pl.ds(c * NB, NB)], pair_sem.at[0, c], pair_sem.at[1, c], partner)

    def moved_pair(c):
        return send(
            final.at[pl.ds(c * NB, NB), 0:PW], moved.at[pl.ds(c * NB, NB)], moved_sem.at[0, c], moved_sem.at[1, c],
            partner,
        )

    def row_copy(c, d):
        where = (lax.rem(row + d, pairs) * 2 + core, place)
        return send(
            pair_in.at[pl.ds(c * NB, NB)], others.at[c, d - 1], row_sem.at[0, c], row_sem.at[1, c], where
        )

    def moved_copy(c, d):
        where = (lax.rem(row + d, pairs) * 2 + core, place)
        into = moved.at[pl.ds(c * NB, NB)]
        return send(into, into, moved_sem.at[2, c], moved_sem.at[1, c], where)

    def goal_of(k):
        goal, c = x_where(k)
        return goal, c, goal * 2 + side, goal * per + c

    def x_part(k):
        goal, c, owner, slot = goal_of(k)

        @pl.when(owner >= owners)
        def _():
            x_copy(k)[1].wait_recv()
            at = pl.multiple_of(owner * cols + c * NB, NB)
            xr[k] = xr[k] + dense[pl.ds(at, NB), :]

            @pl.when((level < goal) & (level == 0))
            def _():
                z_copy(k, 1).start()

            @pl.when((level > goal) & (level == depth - 1))
            def _():
                z_copy(k, -1).start()

    def z_part(k):
        goal, c, owner, slot = goal_of(k)

        @pl.when(owner >= owners)
        def _():
            @pl.when((level <= goal) & (level > 0))
            def _():
                pltpu.make_async_copy(zl.at[slot], zl.at[slot], z_sem.at[1, slot]).wait()
                xr[k] = xr[k] + zl[slot]

            @pl.when((level >= goal) & (level < depth - 1))
            def _():
                pltpu.make_async_copy(zr.at[slot], zr.at[slot], z_sem.at[2, slot]).wait()
                xr[k] = xr[k] + zr[slot]

            @pl.when((level < goal) & (level > 0))
            def _():
                z_copy(k, 1).start()

            @pl.when((level > goal) & (level < depth - 1))
            def _():
                z_copy(k, -1).start()

            if k >= steps - per:
                final[c * NB : c * NB + NB, :] = xr[k]
                mine[c * NB : c * NB + NB, :] = hdot(xr[k], pick[...])
                pair_copy(c).start()
                pl.when(group == 0)(moved_pair(c).start)

    def row_part(c):
        @pl.when(place >= owners)
        def _():
            lo = c * NB
            pair_copy(c).wait()
            pair_in[lo : lo + NB, :] = pair_in[lo : lo + NB, :] + mine[lo : lo + NB, :]
            for d in range(1, pairs):
                row_copy(c, d).start()

            @pl.when(group == 0)
            def _():
                moved[lo : lo + NB, :] = final[lo : lo + NB, 0:PW]

            @pl.when(group == 1)
            def _():
                local(moved.at[pl.ds(lo, NB)], moved_sem.at[1, c]).wait()

            @pl.when(row == 0)
            def _():
                for d in range(1, pairs):
                    moved_copy(c, d).start()

    x_part(0)
    kept = (reducers - 1) * piece
    local(diag.at[pl.ds(0, kept)], diag_sem.at[5]).wait()
    if_not_reducer(lambda: local(diag.at[pl.ds(0, piece)], diag_sem.at[5]).wait())
    for d in range(1, n_row):
        own = rows_of(diag, group * wide, wide)
        send(own, own, diag_sem.at[6], diag_sem.at[7], (lax.rem(group + d, n_row), place)).start()
    x_send(3)
    x_send(4)
    panel_sum()
    x_part(1)
    x_part(2)
    local(diag.at[pl.ds(0, (n_row - 1) * wide)], diag_sem.at[7]).wait()
    packed[...] = diag[...]
    x_send(5)
    work = factor(packed, low_inv, up_inv)
    head = group == 0
    hit = hdot_t(jnp.ones((8, PW), F32), pick[...])[0:1, :] > 0.5

    def solve_x():
        @pl.when(group > 0)
        def _():
            local(lead, lead_sem.at[1, 0]).wait()

        @pl.when(group == 0)
        def _():
            lead[...] = panel[:, 0:PW]

        x[...] = jnp.where(hit, hdot_t(lead[...], pick[...]), panel[...])
        x[:, 0:PW] = jnp.where(head, diag[...], x[:, 0:PW])
        for s in range(0, PW, B):
            e = s + B
            term = x[s:e, :]
            if s:
                term = term - hdot(packed[s:e, 0:s], x[0:s, :])
            x[s:e, :] = hdot(low_inv[s:e, :], term)

    def finish(begin, end):
        @pl.when(place >= owners)
        def _():
            for c in range(begin, end):
                lo = c * NB
                local(others.at[c], row_sem.at[1, c]).wait()

                @pl.when(row > 0)
                def _():
                    local(moved.at[pl.ds(lo, NB)], moved_sem.at[1, c]).wait()

                mine[lo : lo + NB, :] = pair_in[lo : lo + NB, :] + jnp.sum(others[c], axis=0)
            lo, hi = begin * NB, end * NB
            for s in range(0, PW, B):
                e = s + B
                term = mine[lo:hi, s:e]
                if s:
                    term = term - hdot(y[lo:hi, 0:s], packed[0:s, s:e])
                y[lo:hi, s:e] = hdot(term, up_inv[s:e, :])
            swapped = jnp.where(hit, hdot_t(moved[lo:hi, :], pick[...]), final[lo:hi, :])
            out[lo:hi, :] = swapped - hdot(y[lo:hi, :], x[...])
            out[lo:hi, 0:PW] = jnp.where(head, y[lo:hi, :], out[lo:hi, 0:PW])

    first = 3
    far = near * per
    total = (B // 4 + 1) * (PW // B)
    pace = -(-total // (steps - first - per))
    for k in range(first, steps):
        x_part(k)
        if k - LAG < far:
            z_part(k - LAG)
        if k >= far:
            z_part(k)
        x_send(k + LAG)
        if k > steps - per:
            row_part(k - steps + per - 1)
        if k == 5:
            panel_gather()
        if k == 8:
            panel_finish()
        for _ in range(pace):
            next(work, None)
        if k == steps - 2:
            for _ in work:
                pass
            solve_x()
    row_part(per - 1)
    if per > 1:
        finish(0, per - 1)
    finish(per - 1, per)

    @pl.when(place < owners)
    def _():
        x[:, 0:PW] = jnp.where(head, packed[...], x[:, 0:PW])
        off = pl.multiple_of(lax.rem(place, owners) * cols, cols)
        out[...] = x[pl.ds(off, cols), :]

    local(block_in, diag_sem.at[0]).wait()
    local(block.at[pl.ds(0, kept)], diag_sem.at[2]).wait()
    if_not_reducer(lambda: local(block.at[pl.ds(0, piece)], diag_sem.at[2]).wait())
    if_reducer(lambda: local(piece_in, diag_sem.at[4]).wait())
    local(block_in, diag_sem.at[6]).wait()
    half_copy.wait_send()
    local(part_in, panel_sem.at[2]).wait()
    local(part_in, panel_sem.at[4]).wait()
    panel_twin(part_at).wait_send()
    local(part_in, panel_sem.at[8]).wait()

    @pl.when(group == 0)
    def _():
        for d in range(1, n_row):
            lead_copy(d).wait_send()

    for k in range(steps):
        live, copy = x_copy(k)
        pl.when(live)(copy.wait_send)
        goal, c, owner, slot = goal_of(k)

        @pl.when((owner >= owners) & (level != goal))
        def _():
            z_copy(k, 1).wait_send()

    @pl.when(place >= owners)
    def _():
        for c in range(per):
            local(others.at[c], row_sem.at[0, c]).wait()
            pl.when(group == 0)(moved_pair(c).wait_send)

            @pl.when(row == 0)
            def _():
                local(others.at[c], moved_sem.at[2, c]).wait()


def stay(array):
    return pltpu.with_memory_space_constraint(array, pltpu.MemorySpace.HBM)


def shape(*dims):
    return jax.ShapeDtypeStruct(dims, F32)


HBM_SPEC = pl.BlockSpec(memory_space=pltpu.MemorySpace.HBM)
VMEM_SPEC = pl.BlockSpec(memory_space=pltpu.VMEM)
DMA = pltpu.SemaphoreType.DMA


def per_device(
    n_row, n_col, matrix_slab, contributions, target_column, target_rows, live_rows, pivot_index
):
    cols, rows = matrix_slab.shape
    slab_cols = cols * n_col
    count = contributions.shape[1]
    parts = 4
    table = pltpu.SMEM((1, count), jnp.int32)
    dense, sel = pl.pallas_call(
        spread_kernel,
        out_shape=(shape(slab_cols, rows), shape(PW, PW)),
        in_specs=[HBM_SPEC] * 6,
        out_specs=(VMEM_SPEC,) * 2,
        scratch_shapes=[table] * 3
        + [
            VMEM((count, NB, TR), F32),
            VMEM((cols, rows), F32),
            VMEM((1, PW), jnp.int32),
            DMA((5 + parts,)),
        ],
        compiler_params=pltpu.CompilerParams(vmem_limit_bytes=32 * 1024 * 1024),
    )(*map(stay, (target_column, target_rows, live_rows, contributions, matrix_slab, pivot_index)))
    wide = PW // n_row
    piece = max(8, wide // n_col)
    per = cols // NB
    depth = n_col // 2
    steps = depth * per
    part = PW // n_col
    scratch = [
        VMEM((n_row - 1, wide, PW), F32),
        VMEM((wide, PW), F32),
        VMEM((n_col - 1, piece, PW), F32),
        VMEM((PW, PW), F32),
        VMEM((PW // 2, rows), F32),
        VMEM((depth - 1, part, rows), F32),
        VMEM((PW, rows), F32),
        VMEM((PW, PW), F32),
        VMEM((steps, NB, rows), F32),
        VMEM((steps, NB, rows), F32),
        VMEM((steps, NB, rows), F32),
        VMEM((cols, rows), F32),
        VMEM((cols, PW), F32),
        VMEM((cols, PW), F32),
        VMEM((per, n_row // 2 - 1, NB, PW), F32),
        VMEM((cols, PW), F32),
        VMEM((rows, PW), F32),
        VMEM((PW, PW), F32),
        VMEM((PW, B), F32),
        VMEM((PW, B), F32),
        VMEM((PW, rows), F32),
        VMEM((cols, PW), F32),
        VMEM((1, PW), jnp.int32),
        DMA,
        DMA((8,)),
        DMA((10,)),
        DMA((2, n_row)),
        DMA((2, steps)),
        DMA((3, steps)),
        DMA((2, per)),
        DMA((2, per)),
        DMA((3, per)),
    ]
    return pl.pallas_call(
        functools.partial(main_kernel, n_row, n_col),
        out_shape=shape(cols, rows),
        in_specs=[HBM_SPEC] + [VMEM_SPEC] * 2,
        out_specs=VMEM_SPEC,
        scratch_shapes=scratch,
        compiler_params=pltpu.CompilerParams(
            collective_id=0, has_side_effects=True, vmem_limit_bytes=32 * 1024 * 1024
        ),
    )(stay(pivot_index), dense, sel)


def solution(mesh):
    placed = (
        P("pcol", "prow"),
        P("prow", "pcol", None, None),
        P("prow", "pcol"),
        P("prow", "pcol"),
        P("prow", "pcol"),
        P(),
    )
    body = functools.partial(per_device, mesh.shape["prow"], mesh.shape["pcol"])

    def whole(*args):
        return jax.shard_map(
            body, mesh=mesh, in_specs=placed, out_specs=P("pcol", "prow"), check_vma=False
        )(*args)

    return whole
```

time: 106 us -> 78.8 us (0.74)
  the two profiles are of different devices: /device:TPU:2 before, /device:TPU:23 now
where the time goes in v2:
time: 78.8 us; the launch traced here: 77.6 us
  Pallas kernels  76.8 us (97%)
  local copies, waits for them, and re-layouts  0.8 us (1%)
    pallas_call x1, Pallas kernels, per_device(): pl.pallas_call(functools.partial(main_kernel, n_row, n_col), out_shape=sh...  74.3 us
    pallas_call x1, Pallas kernels, per_device(): pl.pallas_call(spread_kernel, out_shape=(shape(slab_cols, rows), shape(PW...  2.51 us

profile of v2, /device:TPU:23, one launch (start us, length us, event | category | flops | bytes accessed | tf_op | source)
XLA Modules:
  0.0 77.6 jit_solution(2315788600415393094)
XLA Ops:
  0.0 2.5 %shard_map.64 = (f32[2048,512]{1,0:T(8,128)S(1)}, f32[256,256]{1,0:T(8,128)S(1)}) custom-call(s32[1,32]{1,0:T(1,128)} %tc.1, s32[1,32]{1,0:T(1,128)} %tr.1, s32[1,32]{1,0:T(1,128)} %lr.1, f32[1,32,64,256]{3,2,1,0:T(8,128)} %blocks.1, f32[256,512]{1,0:T(8,128)} %slab.1, s32[1,256]{1,0:T(1,128)} %pivots.3), custom_call_target="tpu_custom_call" | custom-call | tf_op jit(solution)/shard_map/pallas_call | solution.py:550
  2.5 74.3 %shard_map.65 = f32[256,512]{1,0:T(8,128)S(1)} custom-call(s32[1,256]{1,0:T(1,128)} %pivots.3, f32[2048,512]{1,0:T(8,128)S(1)} %get-tuple-element.7.dense, f32[256,256]{1,0:T(8,128)S(1)} %get-tuple-element.8.sel), custom_call_target="tpu_custom_call" | custom-call | tf_op jit(solution)/shard_map/pallas_call | solution.py:604
  76.8 0.8 %copy.8 = f32[256,512]{1,0:T(8,128)} copy(f32[256,512]{1,0:T(8,128)S(1)} %shard_map.65) | data formatting | bytes 1048576

commit v3 on v2

--- a/solution.py
+++ b/solution.py
@@ -11,7 +11,9 @@
 NB = 64
 TR = 256
 B = 64
-LAG = 3
+LAG = 2
+AHEAD = 4
+PACE = 8
 
 HIGHEST = lax.Precision.HIGHEST
 VMEM = pltpu.VMEM
@@ -120,9 +122,9 @@
 def main_kernel(
     n_row, n_col,
     pivots, dense, sel, out,
-    block_in, block, piece_in, diag, half_in, part_in, panel, lead, xr, zl, zr,
-    final, mine, pair_in, others, moved, pick, packed, low_inv, up_inv, x, y,
-    pivot_row, pivot_sem, diag_sem, panel_sem, lead_sem, x_sem, z_sem, pair_sem, row_sem, moved_sem,
+    block_in, block, piece_in, diag, level_in, level_sum, twin_in, band_sum, lead, xr, zl, zr,
+    final, mine, pair_in, others, moved, pick, packed, low_inv, up_inv, x, y, inverse,
+    pivot_row, pivot_sem, diag_sem, panel_sem, lead_sem, chain_sem, x_sem, z_sem, pair_sem, row_sem, moved_sem,
 ):
     cols, rows = out.shape
     group, place = lax.axis_index("prow"), lax.axis_index("pcol")
@@ -135,7 +137,7 @@
     reducers = wide // piece
     pairs = n_row // 2
     depth = n_col // 2
-    part = part_in.shape[1]
+    band = twin_in.shape[0]
     steps = depth * per
     level, side = lax.div(place, 2), lax.rem(place, 2)
     row, core = lax.div(group, 2), lax.rem(group, 2)
@@ -169,22 +171,34 @@
     lax.fori_loop(1, n, greet, 0)
     pivot_copy.wait()
     pick[...] = pick_matrix(pivot_row, group, rows)
+    head = group == 0
+    hit = hdot_t(jnp.ones((8, PW), F32), pick[...])[0:1, :] > 0.5
     pl.semaphore_wait(barrier, n - 1)
 
     for d in range(1, n_row):
         t = lax.rem(group + d, n_row)
         send(rows_of(sel, t * wide, wide), block_in.at[d - 1], diag_sem.at[0], diag_sem.at[1], (t, place)).start()
-    keep = PW // 2
-    half_copy = send(
-        rows_of(dense, (1 - side) * keep, keep), half_in, panel_sem.at[0], panel_sem.at[1], across
-    )
-    half_copy.start()
+    def level_send(d):
+        t = lax.rem(level + d, depth)
+        send(
+            rows_of(dense, t * band, band), level_in.at[d - 1], panel_sem.at[0], panel_sem.at[1],
+            (group, t * 2 + side),
+        ).start()
 
     def x_where(k):
         zone, c = divmod(k, per)
-        if zone < near:
-            return half * zone + (1 - half) * (depth - 1 - zone), c
-        return half * near + lax.rem(level - half * near + 1 + zone - near, near), c
+
+        def far_goal(i):
+            return half * i + (1 - half) * (depth - 1 - i)
+
+        def near_goal(i):
+            return half * near + lax.rem(level - half * near + 1 + i, near)
+
+        goal = far_goal(zone) if zone < near else near_goal(zone - near)
+        if near == 2 and zone in (1, 2):
+            edge = 1 - lax.rem(lax.div(level + 1, 2), 2)
+            goal = edge * goal + (1 - edge) * (near_goal(0) if zone == 1 else far_goal(1))
+        return goal, c
 
     def x_copy(k):
         goal, c = x_where(k)
@@ -207,6 +221,8 @@
         if reducers != n_col:
             pl.when(place >= reducers)(f)
 
+    level_send(1)
+    x_send(0)
     local(block_in, diag_sem.at[1]).wait()
     at = pl.multiple_of(group * wide, wide)
     block[...] = sel[pl.ds(at, wide), :] + jnp.sum(block_in[...], axis=0)
@@ -226,58 +242,77 @@
         return carry
 
     lax.fori_loop(1, n_col, piece_send, 0)
-    x_send(0)
-
-    def panel_middle():
-        half_copy.wait_recv()
-        at = pl.multiple_of(side * keep, keep)
-        half_in[...] = half_in[...] + dense[pl.ds(at, keep), :]
-        for d in range(1, depth):
-            t = lax.rem(level + d, depth)
-            send(
-                rows_of(half_in, t * part, part), part_in.at[d - 1], panel_sem.at[2], panel_sem.at[3],
-                (group, t * 2 + side),
-            ).start()
-
-    part_at = pl.multiple_of(side * keep + level * part, part)
-    twin_at = pl.multiple_of((1 - side) * keep + level * part, part)
+    level_send(depth - 1)
+    x_send(1)
+    own_band = pl.multiple_of(level * band, band)
+
+    def twin_copy():
+        return send(level_sum, twin_in, panel_sem.at[2], panel_sem.at[3], across)
 
     def panel_sum():
-        local(part_in, panel_sem.at[3]).wait()
-        mid = pl.multiple_of(level * part, part)
-        panel[pl.ds(part_at, part), :] = half_in[pl.ds(mid, part), :] + jnp.sum(part_in[...], axis=0)
-        panel_twin(part_at).start()
-        panel_spread(part_at, 4)
-
-    def panel_twin(at):
-        own = panel.at[pl.ds(at, part)]
-        return send(own, own, panel_sem.at[6], panel_sem.at[7], across)
-
-    def panel_spread(at, sem):
-        own = panel.at[pl.ds(at, part)]
-        for d in range(1, depth):
-            t = lax.rem(level + d, depth)
-            send(own, own, panel_sem.at[sem], panel_sem.at[sem + 1], (group, t * 2 + side)).start()
-
-    def panel_gather():
-        panel_twin(twin_at).wait_recv()
-        panel_spread(twin_at, 8)
+        local(level_in, panel_sem.at[1]).wait()
+        level_sum[...] = dense[pl.ds(own_band, band), :] + jnp.sum(level_in[...], axis=0)
+        twin_copy().start()
 
     def lead_copy(d):
         return send(
-            panel.at[:, 0:PW], lead, lead_sem.at[0, d], lead_sem.at[1, 0], (lax.rem(group + d, n_row), place)
-        )
-
-    def panel_finish():
-        local(part_in, panel_sem.at[5]).wait()
-        local(part_in, panel_sem.at[9]).wait()
+            band_sum.at[:, 0:PW], lead, lead_sem.at[0, d], lead_sem.at[1, 0], (lax.rem(group + d, n_row), place)
+        )
+
+    def panel_twin():
+        twin_copy().wait_recv()
+        band_sum[...] = level_sum[...] + twin_in[...]
 
         @pl.when(group == 0)
         def _():
             for d in range(1, n_row):
                 lead_copy(d).start()
 
-    panel_middle()
+    def chain_copy(index, way):
+        own = rows_of(x, index * band, band)
+        return send(
+            own, own, chain_sem.at[0 if way > 0 else 1, index], chain_sem.at[2, index], (group, place + 2 * way)
+        )
+
+    def panel_swap():
+        @pl.when(group > 0)
+        def _():
+            local(lead, lead_sem.at[1, 0]).wait()
+
+        @pl.when(group == 0)
+        def _():
+            lead[...] = band_sum[:, 0:PW]
+
+        x[pl.ds(own_band, band), :] = jnp.where(hit, hdot_t(lead[...], pick[...]), band_sum[...])
+        pl.when(level < depth - 1)(chain_copy(level, 1).start)
+        pl.when(level > 0)(chain_copy(level, -1).start)
+
+    def panel_step(s, way, final_stop):
+        index = level - s * way
+        inside = (index >= 0) & (index < depth)
+        index = lax.rem(index + depth, depth)
+        end = (level == depth - 1) if way > 0 else (level == 0)
+
+        @pl.when(inside & (end if final_stop else jnp.logical_not(end)))
+        def _():
+            chain_copy(index, way).wait_recv()
+            if not final_stop:
+                chain_copy(index, way).start()
+
+    def panel_stage(s):
+        for way in (1, -1):
+            panel_step(s, way, False)
+
+    def panel_collect():
+        for s in range(1, depth):
+            for way in (1, -1):
+                panel_step(s, way, True)
+
+    def panel_sent():
+        for b in range(depth):
+            pl.when((b <= level) & (level < depth - 1))(chain_copy(b, 1).wait_send)
+            pl.when((b >= level) & (level > 0))(chain_copy(b, -1).wait_send)
+
     diag_at = pl.multiple_of(group * wide + place * piece, piece)
 
     @if_reducer
@@ -293,7 +328,8 @@
 
         lax.fori_loop(1, n_col, piece_spread, 0)
 
-    x_send(1)
+    for d in range(2, depth - 1):
+        level_send(d)
     x_send(2)
 
     def z_copy(k, way):
@@ -313,6 +349,10 @@
             partner,
         )
 
+    def moved_pass(c):
+        into = moved.at[pl.ds(c * NB, NB)]
+        return send(into, into, moved_sem.at[0, c], moved_sem.at[1, c], partner)
+
     def row_copy(c, d):
         where = (lax.rem(row + d, pairs) * 2 + core, place)
         return send(
@@ -391,40 +431,39 @@
             def _():
                 local(moved.at[pl.ds(lo, NB)], moved_sem.at[1, c]).wait()
 
-            @pl.when(row == 0)
+            @pl.when(group == 0)
             def _():
                 for d in range(1, pairs):
                     moved_copy(c, d).start()
 
-    x_part(0)
     kept = (reducers - 1) * piece
     local(diag.at[pl.ds(0, kept)], diag_sem.at[5]).wait()
     if_not_reducer(lambda: local(diag.at[pl.ds(0, piece)], diag_sem.at[5]).wait())
     for d in range(1, n_row):
         own = rows_of(diag, group * wide, wide)
         send(own, own, diag_sem.at[6], diag_sem.at[7], (lax.rem(group + d, n_row), place)).start()
-    x_send(3)
-    x_send(4)
-    panel_sum()
-    x_part(1)
-    x_part(2)
+    for k in range(3, AHEAD + 1):
+        x_send(k)
+    x_part(0)
     local(diag.at[pl.ds(0, (n_row - 1) * wide)], diag_sem.at[7]).wait()
     packed[...] = diag[...]
-    x_send(5)
-    work = factor(packed, low_inv, up_inv)
-    head = group == 0
-    hit = hdot_t(jnp.ones((8, PW), F32), pick[...])[0:1, :] > 0.5
+
+    def all_work():
+        yield from factor(packed, low_inv, up_inv)
+        inverse[...] = jnp.zeros_like(inverse)
+        for s in range(0, PW, B):
+            e = s + B
+            inverse[s:e, s:e] = up_inv[s:e, :]
+            if s:
+                term = hdot(packed[0:s, s:e], up_inv[s:e, :])
+                inverse[0:s, s:e] = -hdot(inverse[0:s, 0:s], term)
+            yield None
+
+    work = all_work()
 
     def solve_x():
-        @pl.when(group > 0)
-        def _():
-            local(lead, lead_sem.at[1, 0]).wait()
-
-        @pl.when(group == 0)
-        def _():
-            lead[...] = panel[:, 0:PW]
-
-        x[...] = jnp.where(hit, hdot_t(lead[...], pick[...]), panel[...])
+        panel_collect()
+        panel_sent()
         x[:, 0:PW] = jnp.where(head, diag[...], x[:, 0:PW])
         for s in range(0, PW, B):
             e = s + B
@@ -443,46 +482,47 @@
                 @pl.when(row > 0)
                 def _():
                     local(moved.at[pl.ds(lo, NB)], moved_sem.at[1, c]).wait()
+                    pl.when(core == 0)(moved_pass(c).start)
 
                 mine[lo : lo + NB, :] = pair_in[lo : lo + NB, :] + jnp.sum(others[c], axis=0)
             lo, hi = begin * NB, end * NB
-            for s in range(0, PW, B):
-                e = s + B
-                term = mine[lo:hi, s:e]
-                if s:
-                    term = term - hdot(y[lo:hi, 0:s], packed[0:s, s:e])
-                y[lo:hi, s:e] = hdot(term, up_inv[s:e, :])
+            y[lo:hi, :] = hdot(mine[lo:hi, :], inverse[...])
             swapped = jnp.where(hit, hdot_t(moved[lo:hi, :], pick[...]), final[lo:hi, :])
             out[lo:hi, :] = swapped - hdot(y[lo:hi, :], x[...])
             out[lo:hi, 0:PW] = jnp.where(head, y[lo:hi, :], out[lo:hi, 0:PW])
 
-    first = 3
     far = near * per
-    total = (B // 4 + 1) * (PW // B)
-    pace = -(-total // (steps - first - per))
-    for k in range(first, steps):
+    last = steps - per
+    for k in range(1, steps):
+        for s in range(1, depth - 1):
+            if k == (4 + 2 * s if near == 2 else 5):
+                panel_stage(s)
         x_part(k)
-        if k - LAG < far:
+        if 0 <= k - LAG < far:
             z_part(k - LAG)
         if k >= far:
             z_part(k)
-        x_send(k + LAG)
-        if k > steps - per:
-            row_part(k - steps + per - 1)
-        if k == 5:
-            panel_gather()
-        if k == 8:
-            panel_finish()
-        for _ in range(pace):
+        if k == 1:
+            panel_sum()
+            for later in range(AHEAD + 1, steps):
+                x_send(later)
+        if k == 3:
+            panel_twin()
+        if k == 4:
+            panel_swap()
+        for _ in range(PACE):
             next(work, None)
-        if k == steps - 2:
+        if k == min(last + 1, steps - 1):
             for _ in work:
                 pass
             solve_x()
+        if k > last:
+            row_part(k - last - 1)
+        if k > last + 2:
+            finish(k - last - 3, k - last - 2)
     row_part(per - 1)
-    if per > 1:
-        finish(0, per - 1)
-    finish(per - 1, per)
+    for c in range(max(per - 3, 0), per):
+        finish(c, c + 1)
 
     @pl.when(place < owners)
     def _():
@@ -495,11 +535,8 @@
     if_not_reducer(lambda: local(block.at[pl.ds(0, piece)], diag_sem.at[2]).wait())
     if_reducer(lambda: local(piece_in, diag_sem.at[4]).wait())
     local(block_in, diag_sem.at[6]).wait()
-    half_copy.wait_send()
-    local(part_in, panel_sem.at[2]).wait()
-    local(part_in, panel_sem.at[4]).wait()
-    panel_twin(part_at).wait_send()
-    local(part_in, panel_sem.at[8]).wait()
+    local(level_in, panel_sem.at[0]).wait()
+    twin_copy().wait_send()
 
     @pl.when(group == 0)
     def _():
@@ -519,9 +556,9 @@
     def _():
         for c in range(per):
             local(others.at[c], row_sem.at[0, c]).wait()
-            pl.when(group == 0)(moved_pair(c).wait_send)
-
-            @pl.when(row == 0)
+            pl.when(core == 0)(moved_pair(c).wait_send)
+
+            @pl.when(group == 0)
             def _():
                 local(others.at[c], moved_sem.at[2, c]).wait()
 
@@ -566,16 +603,16 @@
     per = cols // NB
     depth = n_col // 2
     steps = depth * per
-    part = PW // n_col
     scratch = [
         VMEM((n_row - 1, wide, PW), F32),
         VMEM((wide, PW), F32),
         VMEM((n_col - 1, piece, PW), F32),
         VMEM((PW, PW), F32),
-        VMEM((PW // 2, rows), F32),
-        VMEM((depth - 1, part, rows), F32),
-        VMEM((PW, rows), F32),
-        VMEM((PW, PW), F32),
+        VMEM((depth - 1, PW // depth, rows), F32),
+        VMEM((PW // depth, rows), F32),
+        VMEM((PW // depth, rows), F32),
+        VMEM((PW // depth, rows), F32),
+        VMEM((PW // depth, PW), F32),
         VMEM((steps, NB, rows), F32),
         VMEM((steps, NB, rows), F32),
         VMEM((steps, NB, rows), F32),
@@ -590,11 +627,13 @@
         VMEM((PW, B), F32),
         VMEM((PW, rows), F32),
         VMEM((cols, PW), F32),
+        VMEM((PW, PW), F32),
         VMEM((1, PW), jnp.int32),
         DMA,
         DMA((8,)),
-        DMA((10,)),
+        DMA((4,)),
         DMA((2, n_row)),
+        DMA((3, depth)),
         DMA((2, steps)),
         DMA((3, steps)),
         DMA((2, per)),

time: 78.8 us -> 75.1 us (0.953); the launches traced: 77.6 us -> 75 us
  Pallas kernels: 76.8 us -> 74.1 us
    pallas_call x1, Pallas kernels: 74.3 us -> 71.6 us  [per_device(): pl.pallas_call(functools.partial(main_kernel, n_row, n_col), out_shape=sh...]
where the time goes in v3:
time: 75.1 us; the launch traced here: 75 us
  Pallas kernels  74.1 us (99%)
  local copies, waits for them, and re-layouts  0.8 us (1%)
    pallas_call x1, Pallas kernels, per_device(): pl.pallas_call(functools.partial(main_kernel, n_row, n_col), out_shape=sh...  71.6 us
    pallas_call x1, Pallas kernels, per_device(): pl.pallas_call(spread_kernel, out_shape=(shape(slab_cols, rows), shape(PW...  2.51 us

profile of v3, /device:TPU:23, one launch (start us, length us, event | category | flops | bytes accessed | tf_op | source)
XLA Modules:
  0.0 75.0 jit_solution(14889778242635142778)
XLA Ops:
  0.0 2.5 %shard_map.64 = (f32[2048,512]{1,0:T(8,128)S(1)}, f32[256,256]{1,0:T(8,128)S(1)}) custom-call(s32[1,32]{1,0:T(1,128)} %tc.1, s32[1,32]{1,0:T(1,128)} %tr.1, s32[1,32]{1,0:T(1,128)} %lr.1, f32[1,32,64,256]{3,2,1,0:T(8,128)} %blocks.1, f32[256,512]{1,0:T(8,128)} %slab.1, s32[1,256]{1,0:T(1,128)} %pivots.3), custom_call_target="tpu_custom_call" | custom-call | tf_op jit(solution)/shard_map/pallas_call | solution.py:587
  2.5 71.6 %shard_map.65 = f32[256,512]{1,0:T(8,128)S(1)} custom-call(s32[1,256]{1,0:T(1,128)} %pivots.3, f32[2048,512]{1,0:T(8,128)S(1)} %get-tuple-element.7.dense, f32[256,256]{1,0:T(8,128)S(1)} %get-tuple-element.8.sel), custom_call_target="tpu_custom_call" | custom-call | tf_op jit(solution)/shard_map/pallas_call | solution.py:643
  74.2 0.8 %copy.8 = f32[256,512]{1,0:T(8,128)} copy(f32[256,512]{1,0:T(8,128)S(1)} %shard_map.65) | data formatting | bytes 1048576

commit v4 on v3

--- a/solution.py
+++ b/solution.py
@@ -13,7 +13,8 @@
 B = 64
 LAG = 2
 AHEAD = 4
-PACE = 8
+EARLY = 3
+PACE = 7
 
 HIGHEST = lax.Precision.HIGHEST
 VMEM = pltpu.VMEM
@@ -331,6 +332,7 @@
     for d in range(2, depth - 1):
         level_send(d)
     x_send(2)
+    x_send(3)
 
     def z_copy(k, way):
         goal, c = x_where(k)
@@ -436,15 +438,17 @@
                 for d in range(1, pairs):
                     moved_copy(c, d).start()
 
+    x_part(0)
     kept = (reducers - 1) * piece
     local(diag.at[pl.ds(0, kept)], diag_sem.at[5]).wait()
     if_not_reducer(lambda: local(diag.at[pl.ds(0, piece)], diag_sem.at[5]).wait())
     for d in range(1, n_row):
         own = rows_of(diag, group * wide, wide)
         send(own, own, diag_sem.at[6], diag_sem.at[7], (lax.rem(group + d, n_row), place)).start()
-    for k in range(3, AHEAD + 1):
+    for k in range(4, AHEAD + 1):
         x_send(k)
-    x_part(0)
+    for k in range(1, EARLY):
+        x_part(k)
     local(diag.at[pl.ds(0, (n_row - 1) * wide)], diag_sem.at[7]).wait()
     packed[...] = diag[...]
 
@@ -497,7 +501,8 @@
         for s in range(1, depth - 1):
             if k == (4 + 2 * s if near == 2 else 5):
                 panel_stage(s)
-        x_part(k)
+        if k >= EARLY:
+            x_part(k)
         if 0 <= k - LAG < far:
             z_part(k - LAG)
         if k >= far:

time: 75.1 us -> 74.2 us (0.988)
  Pallas kernels: 74.1 us -> 72.7 us
    pallas_call x1, Pallas kernels: 71.6 us -> 70.2 us  [per_device(): pl.pallas_call(functools.partial(main_kernel, n_row, n_col), out_shape=sh...]
where the time goes in v4:
time: 74.2 us; the launch traced here: 73.5 us
  Pallas kernels  72.7 us (98%)
  local copies, waits for them, and re-layouts  0.8 us (1%)
    pallas_call x1, Pallas kernels, per_device(): pl.pallas_call(functools.partial(main_kernel, n_row, n_col), out_shape=sh...  70.2 us
    pallas_call x1, Pallas kernels, per_device(): pl.pallas_call(spread_kernel, out_shape=(shape(slab_cols, rows), shape(PW...  2.51 us

profile of v4, /device:TPU:23, one launch (start us, length us, event | category | flops | bytes accessed | tf_op | source)
XLA Modules:
  0.0 73.5 jit_solution(8055455852147129052)
XLA Ops:
  0.0 2.5 %shard_map.64 = (f32[2048,512]{1,0:T(8,128)S(1)}, f32[256,256]{1,0:T(8,128)S(1)}) custom-call(s32[1,32]{1,0:T(1,128)} %tc.1, s32[1,32]{1,0:T(1,128)} %tr.1, s32[1,32]{1,0:T(1,128)} %lr.1, f32[1,32,64,256]{3,2,1,0:T(8,128)} %blocks.1, f32[256,512]{1,0:T(8,128)} %slab.1, s32[1,256]{1,0:T(1,128)} %pivots.3), custom_call_target="tpu_custom_call" | custom-call | tf_op jit(solution)/shard_map/pallas_call | solution.py:592
  2.5 70.2 %shard_map.65 = f32[256,512]{1,0:T(8,128)S(1)} custom-call(s32[1,256]{1,0:T(1,128)} %pivots.3, f32[2048,512]{1,0:T(8,128)S(1)} %get-tuple-element.7.dense, f32[256,256]{1,0:T(8,128)S(1)} %get-tuple-element.8.sel), custom_call_target="tpu_custom_call" | custom-call | tf_op jit(solution)/shard_map/pallas_call | solution.py:648
  72.7 0.8 %copy.8 = f32[256,512]{1,0:T(8,128)} copy(f32[256,512]{1,0:T(8,128)S(1)} %shard_map.65) | data formatting | bytes 1048576
